TPU v7x, 32 devices: a whole 2x2x4 slice. The times are simulated.
32 devices in a mesh: shard: 32 (over z, y, x, core).
Axes of the slice: x: 2, y: 2, z: 4, core: 2. Of those that a mesh axis runs over, the one named last changes fastest.
Arguments:
- lookup_ids: int32 [65536], P('shard'), may hold values from 0 to 524287, as said below
- grad_rows: float32 [65536, 128], P('shard'), may hold values from -6 to 6
- emb_table: float32 [524288, 128], P('shard'), may hold values from -4 to 4
- row_accum: float32 [524288], P('shard'), may hold values from 0.01 to 1
Outputs:
- new_table: float32 [524288, 128], P('shard')
- new_accum: float32 [524288], P('shard')
- looked_up: float32 [65536, 128], P('shard')
Inputs may be any that keep to these rules, and one draw needn't show every extreme that they name: `lookup_ids`: each device's 2048 lookups name exactly 64 rows, repeats counted, in the range of every owner; within an owner's range the row numbers follow a power law, so that a few rows are named very often.
All inputs are finite; a program needn't handle non-finite values.
Results may differ from a plain program's by a relative error of at most 0.00002.
Values sent between devices are 32-bit elements; how exact they have to be, the bound alone decides.
A program may use at most 64 MiB of HBM per device.

v0:
```python
import functools

import jax
import jax.numpy as jnp
from jax import lax
from jax.experimental import pallas as pl
from jax.experimental.pallas import tpu as pltpu
from jax.sharding import PartitionSpec as P

LEARNING_RATE = 0.5
EPSILON = 1e-08
LANES = 128
MIB = 1024 * 1024
TILE = 512
BATCH = 16
F32 = jnp.float32
BF16 = jnp.bfloat16


def split3(x):
    hi = x.astype(BF16)
    rest = x - hi.astype(F32)
    mid = rest.astype(BF16)
    low = (rest - mid.astype(F32)).astype(BF16)
    return hi, mid, low


def dot(a, b):
    return jnp.dot(a, b, preferred_element_type=F32)


def column_of(row):
    return jnp.transpose(jnp.broadcast_to(row, (LANES, LANES)))


def one_hot_bf16(mask):
    return jnp.where(mask, 1.0, 0.0).astype(BF16)


def fill(terms, x, width):
    for i, term in enumerate(split3(x)):
        terms[:, i * width : (i + 1) * width] = term


def joined(x, width):
    return x[:, 0:width] + x[:, width : 2 * width] + x[:, 2 * width : 3 * width]


def columns_of(ref, first, count):
    return jnp.concatenate([column_of(ref[pl.ds(first + i, 1), :]) for i in range(count)], axis=0)


def arrange_kernel(
    peers, rows_dev, ids_ref, grads_ref, pos_ref, send_ids_ref, send_ref, terms,
):
    blocks = ids_ref.shape[0]
    look = blocks * LANES
    per_peer = look // peers
    width = grads_ref.shape[1]
    peer_iota = lax.broadcasted_iota(jnp.int32, (peers, LANES), 0)
    slot_iota = lax.broadcasted_iota(jnp.int32, (LANES, LANES), 0)
    before = one_hot_bf16(slot_iota < lax.broadcasted_iota(jnp.int32, (LANES, LANES), 1))
    base = jnp.zeros((peers, 1), F32)
    low = peer_iota * rows_dev
    owned, ranked = [], []
    pos = []
    for b in range(blocks):
        ids = ids_ref[b : b + 1, :]
        mine = (ids >= low) & (ids < low + rows_dev)
        hot = jnp.where(mine, 1.0, 0.0)
        rank = dot(hot.astype(BF16), before) + base
        rank = jnp.sum(hot * rank, axis=0, keepdims=True).astype(jnp.int32)
        peer = jnp.sum(jnp.where(mine, peer_iota, 0), axis=0, keepdims=True)
        pos.append(peer * per_peer + rank)
        pos_ref[b : b + 1, :] = pos[b]
        base = base + jnp.sum(hot, axis=1, keepdims=True)
        offset = ids - peer * rows_dev
        digits = [offset & 255, (offset >> 8) & 255, offset >> 16]
        owned.append(jnp.concatenate([hot * d.astype(F32) for d in digits], axis=0).astype(BF16))
        ranked.append(one_hot_bf16(slot_iota == rank))
    named = lax.dot_general(
        jnp.concatenate(owned, axis=1),
        jnp.concatenate(ranked, axis=1),
        (((1,), (1,)), ((), ())),
        preferred_element_type=F32,
    ).astype(jnp.int32)
    named = named[0:peers] + named[peers : 2 * peers] * 256 + named[2 * peers : 3 * peers] * 65536
    for p in range(peers):
        send_ids_ref[p] = named[p : p + 1, :]
    fill(terms, grads_ref[...], width)

    @pl.loop(0, look // TILE)
    def _(t):
        start = pl.multiple_of(t * TILE, TILE)
        place = start + lax.broadcasted_iota(jnp.int32, (TILE, LANES), 0)
        pick = jnp.concatenate([one_hot_bf16(place == p) for p in pos], axis=1)
        send_ref[pl.ds(start, TILE), :] = joined(dot(pick, terms[...]), width)


def peer_of(me, step, n):
    return lax.rem(me + n // 2 + step, n)


def meet_all(me, n):
    barrier = pltpu.get_barrier_semaphore()

    def greet(step, carry):
        pl.semaphore_signal(
            barrier,
            inc=1,
            device_id=(lax.rem(me + step, n),),
            device_id_type=pl.DeviceIdType.MESH,
        )
        return carry

    lax.fori_loop(1, n, greet, 0)
    pl.semaphore_wait(barrier, n - 1)


def exchange_kernel(n, count, loads, *refs):
    total = count + loads
    ins, outs = refs[:total], refs[total : 2 * total]
    srcs, dsts = ins[:count], outs[:count]
    send_sem, recv_sem, own_sem = refs[2 * total :]
    me = lax.axis_index("shard")
    own = [
        pltpu.make_async_copy(s.at[me], d.at[me], own_sem.at[i])
        for i, (s, d) in enumerate(zip(srcs, dsts))
    ]
    own += [
        pltpu.make_async_copy(ins[i], outs[i], own_sem.at[i]) for i in range(count, total)
    ]
    for copy in own:
        copy.start()
    meet_all(me, n)

    def remote(i, step):
        peer = lax.rem(me + step, n)
        return pltpu.make_async_remote_copy(
            src_ref=srcs[i].at[peer],
            dst_ref=dsts[i].at[me],
            send_sem=send_sem.at[i, step],
            recv_sem=recv_sem.at[i, step],
            device_id=(peer,),
            device_id_type=pl.DeviceIdType.MESH,
        )

    half = n // 2
    for i in range(count):

        def start(s, carry, i=i):
            remote(i, half + s).start()

            @pl.when(s > 0)
            def _():
                remote(i, half - s).start()

            return carry

        lax.fori_loop(0, half, start, 0)

    def finish(step, carry):
        for i in range(count):
            source = lax.rem(me - step + n, n)
            pltpu.make_async_remote_copy(
                src_ref=srcs[i].at[source],
                dst_ref=dsts[i].at[source],
                send_sem=send_sem.at[i, step],
                recv_sem=recv_sem.at[i, step],
                device_id=(source,),
                device_id_type=pl.DeviceIdType.MESH,
            ).wait_recv()
        return carry

    lax.fori_loop(1, n, finish, 0)

    def drain(step, carry):
        for i in range(count):
            remote(i, step).wait_send()
        return carry

    lax.fori_loop(1, n, drain, 0)
    for copy in own:
        copy.wait()


def exchange(n, collective_id, arrays, loads=()):
    count = len(arrays)
    total = count + len(loads)
    vmem = pl.BlockSpec(memory_space=pltpu.VMEM)
    return pl.pallas_call(
        functools.partial(exchange_kernel, n, count, len(loads)),
        out_shape=[jax.ShapeDtypeStruct(a.shape, a.dtype) for a in (*arrays, *loads)],
        in_specs=[vmem] * count + [pl.BlockSpec(memory_space=pltpu.HBM)] * len(loads),
        out_specs=[vmem] * total,
        scratch_shapes=[
            pltpu.SemaphoreType.DMA((count, n)),
            pltpu.SemaphoreType.DMA((count, n)),
            pltpu.SemaphoreType.DMA((total,)),
        ],
        cost_estimate=pl.CostEstimate(flops=0, bytes_accessed=80 * MIB, transcendentals=0),
        compiler_params=pltpu.CompilerParams(
            collective_id=collective_id, has_side_effects=True, vmem_limit_bytes=16 * MIB
        ),
    )(*arrays, *loads)


def owner_kernel(
    ids_smem, ids_ref, grads_ref, accum_ref, emb_hbm,
    fresh_ref, new_accum_ref, table_hbm,
    table, terms, weights, hi_hot, keep_sem, store_sem,
):
    keep = pltpu.make_async_copy(emb_hbm, table, keep_sem)
    keep.start()
    blocks = ids_ref.shape[0]
    look = blocks * LANES
    width = grads_ref.shape[1]
    groups = accum_ref.shape[0]
    fill(terms, grads_ref[...], width)
    terms[:, 3 * width : 4 * width] = jnp.ones((look, width), BF16)
    rows = [ids_ref[b : b + 1, :] for b in range(blocks)]
    acc3 = jnp.concatenate(split3(accum_ref[...]), axis=1)
    lane = lax.broadcasted_iota(jnp.int32, (TILE, LANES), 1)
    group_iota = lax.broadcasted_iota(jnp.int32, (TILE, groups), 1)

    @pl.loop(0, look // TILE)
    def _(t):
        start = pl.multiple_of(t * TILE, TILE)
        here = pl.ds(start, TILE)
        col = columns_of(ids_ref, t * (TILE // LANES), TILE // LANES)
        same = jnp.concatenate([one_hot_bf16(col == r) for r in rows], axis=1)
        out = dot(same, terms[...])
        summed = joined(out, width)
        times = out[:, 3 * width : 3 * width + 1]
        mean = jnp.sum(summed * summed, axis=1, keepdims=True) * (1.0 / width)
        at_lane = (col & (LANES - 1)) == lane
        at_group = one_hot_bf16((col >> 7)[:, 0:1] == group_iota)
        found = joined(dot(at_group, acc3), LANES)
        new_acc = jnp.sum(jnp.where(at_lane, found, 0.0), axis=1, keepdims=True) + mean
        rate = LEARNING_RATE / (jnp.sqrt(new_acc) + EPSILON)
        fresh_ref[here, :] = summed * rate
        share = jnp.where(at_lane, jnp.broadcast_to(mean / times, (TILE, LANES)), 0.0)
        for i, term in enumerate(split3(share)):
            weights[here, i * LANES : (i + 1) * LANES] = term
        hi_hot[here, :] = at_group

    keep.wait()

    @pl.loop(0, look // LANES)
    def _(b):
        start = pl.multiple_of(b * LANES, LANES)
        for i in range(0, LANES, BATCH):
            batch = [table[pl.ds(ids_smem[start + i + k], 1), :] for k in range(BATCH)]
            steps = [fresh_ref[pl.ds(start + i + k, 1), :] for k in range(BATCH)]
            for k in range(BATCH):
                fresh_ref[pl.ds(start + i + k, 1), :] = batch[k] - steps[k]

    @pl.loop(0, look // LANES)
    def _(b):
        start = pl.multiple_of(b * LANES, LANES)
        for i in range(0, LANES, BATCH):
            batch = [fresh_ref[pl.ds(start + i + k, 1), :] for k in range(BATCH)]
            for k in range(BATCH):
                table[pl.ds(ids_smem[start + i + k], 1), :] = batch[k]

    store = pltpu.make_async_copy(table, table_hbm, store_sem)
    store.start()
    added = lax.dot_general(
        hi_hot[...], weights[...], (((0,), (0,)), ((), ())), preferred_element_type=F32
    )
    new_accum_ref[...] = accum_ref[...] + joined(added, LANES)
    store.wait()


def restore_kernel(pos_ref, back_ref, out_ref, terms):
    blocks = pos_ref.shape[0]
    width = back_ref.shape[1]
    fill(terms, back_ref[...], width)
    lane = lax.broadcasted_iota(jnp.int32, (TILE, LANES), 1)

    @pl.loop(0, blocks * LANES // TILE)
    def _(t):
        col = columns_of(pos_ref, t * (TILE // LANES), TILE // LANES)
        pick = jnp.concatenate(
            [one_hot_bf16(col == lane + k * LANES) for k in range(blocks)], axis=1
        )
        here = pl.ds(pl.multiple_of(t * TILE, TILE), TILE)
        out_ref[here, :] = joined(dot(pick, terms[...]), width)


def on_device(lookup_ids, grad_rows, emb_table, row_accum):
    n = lax.axis_size("shard")
    look, width = grad_rows.shape
    rows_dev = emb_table.shape[0]
    per_peer = look // n
    blocks = look // LANES
    groups = rows_dev // LANES
    vmem = pl.BlockSpec(memory_space=pltpu.VMEM)
    smem = pl.BlockSpec(memory_space=pltpu.SMEM)
    anywhere = pl.BlockSpec(memory_space=pl.ANY)

    pos, send_ids, send = pl.pallas_call(
        functools.partial(arrange_kernel, n, rows_dev),
        out_shape=[
            jax.ShapeDtypeStruct((blocks, LANES), jnp.int32),
            jax.ShapeDtypeStruct((n, 1, LANES), jnp.int32),
            jax.ShapeDtypeStruct((look, width), F32),
        ],
        in_specs=[vmem, vmem],
        out_specs=[vmem] * 3,
        scratch_shapes=[
            pltpu.VMEM((look, 3 * width), BF16),
        ],
        compiler_params=pltpu.CompilerParams(vmem_limit_bytes=16 * MIB),
    )(lookup_ids.reshape(blocks, LANES), grad_rows)

    recv_ids, recv = exchange(n, 1, (send_ids, send.reshape(n, per_peer, width)))
    local_ids = recv_ids[:, 0, :per_peer].reshape(look)

    fresh, new_accum, new_table = pl.pallas_call(
        owner_kernel,
        out_shape=[
            jax.ShapeDtypeStruct((look, width), F32),
            jax.ShapeDtypeStruct((groups, LANES), F32),
            jax.ShapeDtypeStruct((rows_dev, width), F32),
        ],
        in_specs=[smem, vmem, vmem, vmem, anywhere],
        out_specs=[vmem, vmem, anywhere],
        scratch_shapes=[
            pltpu.VMEM((rows_dev, width), F32),
            pltpu.VMEM((look, 4 * width), BF16),
            pltpu.VMEM((look, 3 * LANES), BF16),
            pltpu.VMEM((look, groups), BF16),
            pltpu.SemaphoreType.DMA(()),
            pltpu.SemaphoreType.DMA(()),
        ],
        cost_estimate=pl.CostEstimate(flops=0, bytes_accessed=30 * MIB, transcendentals=0),
        compiler_params=pltpu.CompilerParams(vmem_limit_bytes=48 * MIB),
    )(
        local_ids,
        local_ids.reshape(blocks, LANES),
        recv.reshape(look, width),
        row_accum.reshape(groups, LANES),
        emb_table,
    )

    (back,) = exchange(n, 2, (fresh.reshape(n, per_peer, width),))

    looked_up = pl.pallas_call(
        restore_kernel,
        out_shape=jax.ShapeDtypeStruct((look, width), F32),
        in_specs=[vmem, vmem],
        out_specs=vmem,
        scratch_shapes=[pltpu.VMEM((look, 3 * width), BF16)],
        compiler_params=pltpu.CompilerParams(vmem_limit_bytes=24 * MIB),
    )(pos, back.reshape(look, width))
    return (new_table, new_accum.reshape(rows_dev), looked_up)


def solution(mesh):
    in_specs = (P("shard"), P("shard", None), P("shard", None), P("shard"))
    out_specs = (P("shard", None), P("shard"), P("shard", None))
    return jax.shard_map(
        on_device, mesh=mesh, in_specs=in_specs, out_specs=out_specs, check_vma=False
    )
```

profile of v0, /device:TPU:0, one launch (start us, length us, event | category | flops | bytes accessed | tf_op | source)
XLA Modules:
  0.0 94.6 jit_solution(7283027587857127140)
XLA Ops:
  0.6 0.0 copy-start
  0.6 1.2 %copy-done = f32[2048,128]{1,0:T(8,128)S(1)} copy-done((f32[2048,128]{1,0:T(8,128)S(1)}, f32[2048,128]{1,0:T(8,128)}, u32[]{:S(2)}) %copy-start) | copy-done | bytes 1048600
  1.9 0.0 copy-start.2
  1.9 0.7 copy-done.2
  2.6 6.0 %shard_map.67 = (s32[16,128]{1,0:T(8,128)S(1)}, s32[32,1,128]{2,1,0:T(1,128)S(1)}, f32[2048,128]{1,0:T(8,128)S(1)}) custom-call(s32[16,128]{1,0:T(8,128)S(1)} %bitcast.13, f32[2048,128]{1,0:T(8,128)S(1)} %copy-done), custom_call_target="tpu_custom_call" | custom-call | tf_op jit(solution)/shard_map/pallas_call | solution.py:302
  8.6 32.0 %shard_map.68 = (s32[32,1,128]{2,1,0:T(1,128)S(1)}, f32[32,64,128]{2,1,0:T(8,128)S(1)}) custom-call(s32[32,1,128]{2,1,0:T(1,128)S(1)} %get-tuple-element.11.refs_0_, f32[32,64,128]{2,1,0:T(8,128)S(1)} %bitcast.11), custom_call_target="tpu_custom_call" | custom-call | bytes 83886080 | tf_op jit(solution)/shard_map/pallas_call | solution.py:191
  40.6 0.1 fusion
  40.6 0.1 reshape_reshape_squeeze.3.ids_ref
  40.7 0.1 reshape_squeeze.3.ids_smem
  40.8 0.0 copy-start.1
  40.8 0.8 copy-done.1
  41.6 17.4 %shard_map.69 = (f32[2048,128]{1,0:T(8,128)S(1)}, f32[128,128]{1,0:T(8,128)}, f32[16384,128]{1,0:T(8,128)}) custom-call(s32[2048]{0:T(1024)S(1)} %reshape_squeeze.3.ids_smem, s32[16,128]{1,0:T(8,128)S(1)} %reshape_reshape_squeeze.3.ids_ref, f32[2048,128]{1,0:T(8,128)S(1)} %bitcast.9, f32[128,128]{1,0:T(8,128)S(1)} %bitcast.12, f32[16384,128]{1,0:T(8,128)} %emb_hbm.1), custom_call_target="tpu_custom_call" | custom-call | bytes 31457280 | tf_op jit(solution)/shard_map/pallas_call | solution.py:320
  59.0 29.0 %shard_map.70 = f32[32,64,128]{2,1,0:T(8,128)S(1)} custom-call(f32[32,64,128]{2,1,0:T(8,128)S(1)} %bitcast.10), custom_call_target="tpu_custom_call" | custom-call | bytes 83886080 | tf_op jit(solution)/shard_map/pallas_call | solution.py:191
  88.1 6.5 %shard_map.71 = f32[2048,128]{1,0:T(8,128)} custom-call(s32[16,128]{1,0:T(8,128)S(1)} %get-tuple-element.17.pos_ref, f32[2048,128]{1,0:T(8,128)S(1)} %bitcast.8), custom_call_target="tpu_custom_call" | custom-call | tf_op jit(solution)/shard_map/pallas_call | solution.py:349
Async XLA Ops:
  0.6 1.2 %copy-start = (f32[2048,128]{1,0:T(8,128)S(1)}, f32[2048,128]{1,0:T(8,128)}, u32[]{:S(2)}) copy-start(f32[2048,128]{1,0:T(8,128)} %grads_ref.1) | copy-start | bytes 3145732
  1.9 0.7 copy-start.2
  40.8 0.8 copy-start.1
where the time goes:
time: 94.9 us; the launch traced here: 94.6 us
  Pallas kernels  91 us (96%)
  local copies, waits for them, and re-layouts  2.95 us (3%)
    pallas_call x2, Pallas kernels, exchange(): pl.pallas_call(functools.partial(exchange_kernel, n, count, len(loads)),...  61 us
    pallas_call x1, Pallas kernels, on_device(): pl.pallas_call(owner_kernel, out_shape=[jax.ShapeDtypeStruct((look, width...  17.4 us
    pallas_call x1, Pallas kernels, on_device(): pl.pallas_call(restore_kernel, out_shape=jax.ShapeDtypeStruct((look, widt...  6.54 us
    pallas_call x1, Pallas kernels, on_device(): pl.pallas_call(functools.partial(arrange_kernel, n, rows_dev), out_shape=...  6.04 us
    unnamed x6, local copies, waits for them, and re-layouts  2.76 us

commit v1 on v0

v1 whole, which is shorter than its diff:
```python
import functools

import jax
import jax.numpy as jnp
from jax import lax
from jax.experimental import pallas as pl
from jax.experimental.pallas import tpu as pltpu
from jax.sharding import PartitionSpec as P

LEARNING_RATE = 0.5
EPSILON = 1e-08
LANES = 128
MIB = 1024 * 1024
BATCH = 16
MESH = pl.DeviceIdType.MESH
F32 = jnp.float32
BF16 = jnp.bfloat16


def split3(x):
    hi = x.astype(BF16)
    rest = x - hi.astype(F32)
    mid = rest.astype(BF16)
    low = (rest - mid.astype(F32)).astype(BF16)
    return hi, mid, low


def dot(a, b):
    return jnp.dot(a, b, preferred_element_type=F32)


def column_of(row):
    return jnp.transpose(jnp.broadcast_to(row, (LANES, LANES)))


def one_hot_bf16(mask):
    return jnp.where(mask, 1.0, 0.0).astype(BF16)


def fill(terms, x, width):
    for i, term in enumerate(split3(x)):
        terms[:, i * width : (i + 1) * width] = term


def joined(x, width):
    return x[:, 0:width] + x[:, width : 2 * width] + x[:, 2 * width : 3 * width]


def quarter_at(half, inner):
    return inner * (1 + half) + (1 - inner) * 3 * half


def greet_all(barrier, me, n):
    def greet(step, carry):
        pl.semaphore_signal(
            barrier, inc=1, device_id=(lax.rem(me + step, n),), device_id_type=MESH
        )
        return carry

    lax.fori_loop(1, n, greet, 0)


def step_kernel(
    n, ids_hbm, grads_hbm, accum_hbm, emb_hbm,
    pos_ref, ids_ref, fresh, new_accum_ref, table, back,
    lookups, grads, accum, send_ids, send, recv_ids, recv, sorted_terms, terms, acc, cols, old_rows,
    weights, hi_hot, ids_smem,
    load_sem, smem_sem, ids_out, ids_in, grads_out, grads_in, back_out, back_in,
):
    blocks = lookups.shape[0]
    look = blocks * LANES
    width = grads.shape[1]
    rows_dev = table.shape[0]
    groups = accum.shape[0]
    per_peer = look // n
    per_row = LANES // per_peer
    quarter = n // 4
    eighth = n // 8
    piece = look // 8
    tile = look // 4
    me = lax.axis_index("shard")
    side = me // (n // 2)
    loads = [
        pltpu.make_async_copy(s, d, load_sem.at[i])
        for i, (s, d) in enumerate(
            ((ids_hbm, lookups), (grads_hbm, grads), (accum_hbm, accum), (emb_hbm, table))
        )
    ]
    for load in loads:
        load.start()
    barrier = pltpu.get_barrier_semaphore()
    greet_all(barrier, me, n)

    loads[0].wait()
    peer_iota = lax.broadcasted_iota(jnp.int32, (n, LANES), 0)
    slot_iota = lax.broadcasted_iota(jnp.int32, (LANES, LANES), 0)
    before = one_hot_bf16(slot_iota < lax.broadcasted_iota(jnp.int32, (LANES, LANES), 1))
    shift = lax.rem(me, per_row) * per_peer
    base = jnp.zeros((n, 1), F32)
    low = peer_iota * rows_dev
    owned, ranked, pos = [], [], []
    for b in range(blocks):
        ids = lookups[b : b + 1, :]
        mine = (ids >= low) & (ids < low + rows_dev)
        hot = jnp.where(mine, 1.0, 0.0)
        rank = dot(hot.astype(BF16), before) + base
        rank = jnp.sum(hot * rank, axis=0, keepdims=True).astype(jnp.int32)
        peer = jnp.sum(jnp.where(mine, peer_iota, 0), axis=0, keepdims=True)
        pos.append(peer * per_peer + rank)
        pos_ref[b : b + 1, :] = pos[b]
        base = base + jnp.sum(hot, axis=1, keepdims=True)
        offset = ids - peer * rows_dev
        digits = [offset & 255, (offset >> 8) & 255, offset >> 16]
        owned.append(jnp.concatenate([hot * d.astype(F32) for d in digits], axis=0).astype(BF16))
        ranked.append(one_hot_bf16(slot_iota == rank + shift))
    named = lax.dot_general(
        jnp.concatenate(owned, axis=1),
        jnp.concatenate(ranked, axis=1),
        (((1,), (1,)), ((), ())),
        preferred_element_type=F32,
    ).astype(jnp.int32)
    named = named[0:n] + named[n : 2 * n] * 256 + named[2 * n : 3 * n] * 65536
    for p in range(n):
        send_ids[p] = named[p : p + 1, :]
    loads[1].wait()
    fill(sorted_terms, grads[...], width)
    pl.semaphore_wait(barrier, n - 1)

    def rows_of(ref, p):
        return ref.at[pl.ds(pl.multiple_of(p * per_peer, 8), per_peer), :]

    def ids_copy(p, source):
        return pltpu.make_async_remote_copy(
            src_ref=send_ids.at[p], dst_ref=recv_ids.at[source],
            send_sem=ids_out.at[p], recv_sem=ids_in.at[source],
            device_id=(p,), device_id_type=MESH,
        )

    def grads_copy(p, source):
        return pltpu.make_async_remote_copy(
            src_ref=rows_of(send, p), dst_ref=rows_of(recv, source),
            send_sem=grads_out.at[p], recv_sem=grads_in.at[source],
            device_id=(p,), device_id_type=MESH,
        )

    def back_copy(p, source):
        return pltpu.make_async_remote_copy(
            src_ref=rows_of(fresh, p), dst_ref=rows_of(back, source),
            send_sem=back_out.at[p], recv_sem=back_in.at[source],
            device_id=(p,), device_id_type=MESH,
        )

    def first_peer(i):
        cross = 1 - lax.rem(i // 2, 2)
        half = cross * (1 - side) + (1 - cross) * side
        target = quarter_at(half, 1 - i // 4)
        return target * quarter + lax.rem(lax.rem(me, quarter) // eighth + i, 2) * eighth

    def start_piece(copy, i):
        def start(s, carry):
            p = first_peer(i) + lax.rem(lax.rem(me, eighth) + s, eighth)

            @pl.when(p != me)
            def _():
                copy(p, me).start()

            return carry

        lax.fori_loop(0, eighth, start, 0)

    def arrange(i):
        begin = pl.multiple_of(first_peer(i) * per_peer, piece)
        place = begin + lax.broadcasted_iota(jnp.int32, (piece, LANES), 0)
        pick = jnp.concatenate([one_hot_bf16(place == p) for p in pos], axis=1)
        send[pl.ds(begin, piece), :] = joined(dot(pick, sorted_terms[...]), width)

    def start_ids(step, carry):
        ids_copy(lax.rem(me + step, n), me).start()
        return carry

    arrange(0)
    lax.fori_loop(1, n, start_ids, 0)

    @pl.loop(1, 8)
    def _(i):
        arrange(i)
        start_piece(grads_copy, i - 1)

    recv_ids[pl.ds(me, 1)] = send_ids[pl.ds(me, 1)]

    def ids_arrive(step, carry):
        p = lax.rem(me + step, n)
        ids_copy(p, p).wait_recv()
        return carry

    lax.fori_loop(1, n, ids_arrive, 0)
    start_piece(grads_copy, 7)
    rows_of(recv, me)[...] = rows_of(send, me)[...]
    for b in range(blocks):
        ids_ref[b : b + 1, :] = sum(recv_ids[b * per_row + k] for k in range(per_row))
    to_smem = pltpu.make_async_copy(ids_ref, ids_smem, smem_sem)
    to_smem.start()

    @pl.loop(0, blocks)
    def _(b):
        here = pl.ds(pl.multiple_of(b * LANES, LANES), LANES)
        cols[here, :] = column_of(ids_ref[pl.ds(b, 1), :])

    loads[2].wait()
    acc3 = jnp.concatenate(split3(accum[...]), axis=1)
    terms[:, 3 * width : 4 * width] = jnp.ones((tile, width), BF16)
    to_smem.wait()
    loads[3].wait()

    @pl.loop(0, blocks)
    def _(b):
        start = pl.multiple_of(b * LANES, LANES)
        for i in range(0, LANES, BATCH):
            picks = [jnp.clip(ids_smem[b, i + k], 0, rows_dev - 1) for k in range(BATCH)]
            batch = [table[pl.ds(pick, 1), :] for pick in picks]
            for k in range(BATCH):
                old_rows[pl.ds(start + i + k, 1), :] = batch[k]

    acc[...] = jnp.zeros_like(acc)

    @pl.loop(0, 4)
    def _(i):
        half = (i // 2) * (1 - side) + (1 - i // 2) * side
        source = 2 * half + lax.rem(me // quarter + i, 2)

        def arrive(s, carry):
            p = source * quarter + s

            @pl.when(p != me)
            def _():
                grads_copy(p, p).wait_recv()

            return carry

        lax.fori_loop(0, quarter, arrive, 0)
        fill(terms, recv[pl.ds(pl.multiple_of(source * tile, tile), tile), :], width)
        lines = tile // LANES
        rows = [ids_ref[pl.ds(source * lines + k, 1), :] for k in range(lines)]

        @pl.loop(0, 4)
        def _(t):
            here = pl.ds(pl.multiple_of(t * tile, tile), tile)
            col = cols[here, :]
            same = jnp.concatenate([one_hot_bf16(col == r) for r in rows], axis=1)
            acc[here, :] += dot(same, terms[...])

    lane = lax.broadcasted_iota(jnp.int32, (piece, LANES), 1)
    group_iota = lax.broadcasted_iota(jnp.int32, (piece, groups), 1)

    @pl.loop(0, 8)
    def _(i):
        here = pl.ds(pl.multiple_of(first_peer(i) * per_peer, piece), piece)
        col = cols[here, :]
        out = acc[here, :]
        summed = joined(out, width)
        times = out[:, 3 * width : 3 * width + 1]
        mean = jnp.sum(summed * summed, axis=1, keepdims=True) * (1.0 / width)
        at_lane = (col & (LANES - 1)) == lane
        at_group = one_hot_bf16((col >> 7)[:, 0:1] == group_iota)
        found = joined(dot(at_group, acc3), LANES)
        new_acc = jnp.sum(jnp.where(at_lane, found, 0.0), axis=1, keepdims=True) + mean
        rate = LEARNING_RATE / (jnp.sqrt(new_acc) + EPSILON)
        fresh[here, :] = old_rows[here, :] - summed * rate
        share = jnp.where(at_lane, jnp.broadcast_to(mean / times, (piece, LANES)), 0.0)
        for k, term in enumerate(split3(share)):
            weights[here, k * LANES : (k + 1) * LANES] = term
        hi_hot[here, :] = at_group

        @pl.when(i > 0)
        def _():
            start_piece(back_copy, i - 1)

    added = lax.dot_general(
        hi_hot[...], weights[...], (((0,), (0,)), ((), ())), preferred_element_type=F32
    )
    new_accum_ref[...] = accum[...] + joined(added, LANES)
    start_piece(back_copy, 7)
    rows_of(back, me)[...] = rows_of(fresh, me)[...]

    def back_arrive(step, carry):
        p = lax.rem(me + step, n)
        back_copy(p, p).wait_recv()
        return carry

    lax.fori_loop(1, n, back_arrive, 0)

    def drain(step, carry):
        p = lax.rem(me + step, n)
        ids_copy(p, me).wait_send()
        grads_copy(p, me).wait_send()
        back_copy(p, me).wait_send()
        return carry

    lax.fori_loop(1, n, drain, 0)


def finish_kernel(
    pos_smem, ids_smem, fresh, back, accum, table_in,
    new_table, new_accum, looked_up, table,
    rows, table_sem, accum_sem, rows_sem,
):
    del table_in
    look = fresh.shape[0]
    blocks = look // LANES
    tile = look // 4
    keep = pltpu.make_async_copy(accum, new_accum, accum_sem)
    keep.start()

    @pl.loop(0, blocks)
    def _(b):
        start = pl.multiple_of(b * LANES, LANES)
        for i in range(0, LANES, BATCH):
            batch = [fresh[pl.ds(start + i + k, 1), :] for k in range(BATCH)]
            for k in range(BATCH):
                table[pl.ds(ids_smem[b, i + k], 1), :] = batch[k]

    store = pltpu.make_async_copy(table, new_table, table_sem)
    store.start()

    def out_copy(t):
        here = pl.ds(pl.multiple_of(t * tile, tile), tile)
        return pltpu.make_async_copy(rows.at[here, :], looked_up.at[here, :], rows_sem.at[t])

    @pl.loop(0, 4)
    def _(t):
        @pl.loop(0, tile // LANES)
        def _(j):
            b = t * (tile // LANES) + j
            start = pl.multiple_of(b * LANES, LANES)
            for i in range(0, LANES, BATCH):
                batch = [back[pl.ds(pos_smem[b, i + k], 1), :] for k in range(BATCH)]
                for k in range(BATCH):
                    rows[pl.ds(start + i + k, 1), :] = batch[k]

        @pl.when(t > 0)
        def _():
            out_copy(t - 1).start()

    keep.wait()
    out_copy(3).start()
    for t in range(4):
        out_copy(t).wait()
    store.wait()


def in_hbm(x):
    return pltpu.with_memory_space_constraint(x, pltpu.HBM)


def on_device(lookup_ids, grad_rows, emb_table, row_accum):
    n = lax.axis_size("shard")
    look, width = grad_rows.shape
    rows_dev = emb_table.shape[0]
    blocks = look // LANES
    groups = rows_dev // LANES
    vmem = pl.BlockSpec(memory_space=pltpu.VMEM)
    smem = pl.BlockSpec(memory_space=pltpu.SMEM)
    hbm = pl.BlockSpec(memory_space=pltpu.HBM)
    tile = look // 4
    dma = pltpu.SemaphoreType.DMA

    pos, local_ids, fresh, accum, table, back = pl.pallas_call(
        functools.partial(step_kernel, n),
        out_shape=[
            pltpu.VMEM((blocks, LANES), jnp.int32),
            pltpu.VMEM((blocks, LANES), jnp.int32),
            pltpu.VMEM((look, width), F32),
            pltpu.VMEM((groups, LANES), F32),
            pltpu.VMEM((rows_dev, width), F32),
            pltpu.VMEM((look, width), F32),
        ],
        in_specs=[hbm] * 4,
        out_specs=[vmem] * 6,
        scratch_shapes=[
            pltpu.VMEM((blocks, LANES), jnp.int32),
            pltpu.VMEM((look, width), F32),
            pltpu.VMEM((groups, LANES), F32),
            pltpu.VMEM((n, 1, LANES), jnp.int32),
            pltpu.VMEM((look, width), F32),
            pltpu.VMEM((n, 1, LANES), jnp.int32),
            pltpu.VMEM((look, width), F32),
            pltpu.VMEM((look, 3 * width), BF16),
            pltpu.VMEM((tile, 4 * width), BF16),
            pltpu.VMEM((look, 4 * width), F32),
            pltpu.VMEM((look, LANES), jnp.int32),
            pltpu.VMEM((look, width), F32),
            pltpu.VMEM((look, 3 * LANES), BF16),
            pltpu.VMEM((look, groups), BF16),
            pltpu.SMEM((blocks, LANES), jnp.int32),
            dma((4,)),
            dma(()),
            dma((n,)),
            dma((n,)),
            dma((n,)),
            dma((n,)),
            dma((n,)),
            dma((n,)),
        ],
        compiler_params=pltpu.CompilerParams(
            collective_id=1, has_side_effects=True, vmem_limit_bytes=44 * MIB
        ),
    )(
        in_hbm(lookup_ids.reshape(blocks, LANES)),
        in_hbm(grad_rows),
        in_hbm(row_accum.reshape(groups, LANES)),
        in_hbm(emb_table),
    )

    new_table, new_accum, looked_up, _ = pl.pallas_call(
        finish_kernel,
        out_shape=[
            jax.ShapeDtypeStruct((rows_dev, width), F32),
            jax.ShapeDtypeStruct((groups, LANES), F32),
            jax.ShapeDtypeStruct((look, width), F32),
            pltpu.VMEM((rows_dev, width), F32),
        ],
        in_specs=[smem, smem, vmem, vmem, vmem, vmem],
        out_specs=[hbm, hbm, hbm, vmem],
        input_output_aliases={5: 3},
        scratch_shapes=[pltpu.VMEM((look, width), F32), dma(()), dma(()), dma((4,))],
        compiler_params=pltpu.CompilerParams(vmem_limit_bytes=24 * MIB),
    )(pos, local_ids, fresh, back, accum, table)
    return (new_table, new_accum.reshape(rows_dev), looked_up)


def solution(mesh):
    in_specs = (P("shard"), P("shard", None), P("shard", None), P("shard"))
    out_specs = (P("shard", None), P("shard"), P("shard", None))
    return jax.shard_map(
        on_device, mesh=mesh, in_specs=in_specs, out_specs=out_specs, check_vma=False
    )
```

time: 94.9 us -> 68.2 us (0.72)
  Pallas kernels: 91 us -> 67.4 us
  local copies, waits for them, and re-layouts: 2.95 us -> 0 us
    pallas_call x5 -> x2, Pallas kernels: 91 us -> 67.4 us  [the longest x1 61.1 us: on_device(): pl.pallas_call(functools.partial(step_kernel, n), out_shape=[pltpu.VMEM((...]
    unnamed x6 -> x0, local copies, waits for them, and re-layouts: 2.76 us -> none
where the time goes in v1:
time: 68.2 us; the launch traced here: 68 us
  Pallas kernels  67.4 us (99%)
    pallas_call x1, Pallas kernels, on_device(): pl.pallas_call(functools.partial(step_kernel, n), out_shape=[pltpu.VMEM((...  61.1 us
    pallas_call x1, Pallas kernels, on_device(): pl.pallas_call(finish_kernel, out_shape=[jax.ShapeDtypeStruct((rows_dev,...  6.24 us

profile of v1, /device:TPU:0, one launch (start us, length us, event | category | flops | bytes accessed | tf_op | source)
XLA Modules:
  0.0 68.0 jit_solution(11461195343593677290)
XLA Ops:
  0.6 61.1 %shard_map.67 = (s32[16,128]{1,0:T(8,128)S(1)}, s32[16,128]{1,0:T(8,128)S(1)}, f32[2048,128]{1,0:T(8,128)S(1)}, f32[128,128]{1,0:T(8,128)S(1)}, f32[16384,128]{1,0:T(8,128)S(1)}, /*index=5*/f32[2048,128]{1,0:T(8,128)S(1)}) custom-call(s32[16,128]{1,0:T(8,128)} %bitcast.4, f32[2048,128]{1,0:T(8,128)} %grads_hbm.1, f32[128,128]{1,0:T(8,128)} %bitcast.3, ...), custom_call_target="tpu_custom_call" | custom-call | tf_op jit(solution)/shard_map/pallas_call | solution.py:367
  61.8 6.2 %shard_map.68 = (f32[16384,128]{1,0:T(8,128)}, f32[128,128]{1,0:T(8,128)}, f32[2048,128]{1,0:T(8,128)}, f32[16384,128]{1,0:T(8,128)S(1)}) custom-call(s32[16,128]{1,0:T(8,128)S(1)} %get-tuple-element.12.pos_smem, s32[16,128]{1,0:T(8,128)S(1)} %get-tuple-element.13.ids_smem, ...), custom_call_target="tpu_custom_call", output_to_operand_aliasing={{3}: (5, {})} | custom-call | tf_op jit(solution)/shard_map/pallas_call | solution.py:414

commit v2 on v1

--- a/solution.py
+++ b/solution.py
@@ -13,6 +13,17 @@
 MIB = 1024 * 1024
 BATCH = 16
 MESH = pl.DeviceIdType.MESH
+
+
+def order_of(*pieces):
+    return sum(piece * 8**i for i, piece in enumerate(pieces))
+
+
+OUT = order_of(6, 7, 0, 1, 2, 3, 4, 5)
+IN_INNER = order_of(2, 3, 1, 0)
+IN_OUTER = order_of(0, 1, 2, 3)
+BACK_INNER = order_of(4, 6, 0, 5, 7, 1, 2, 3)
+BACK_OUTER = order_of(2, 3, 4, 6, 5, 7, 0, 1)
 F32 = jnp.float32
 BF16 = jnp.bfloat16
 
@@ -80,15 +91,18 @@
     tile = look // 4
     me = lax.axis_index("shard")
     side = me // (n // 2)
+    floor = me // quarter
+    inner = lax.rem(floor + side, 2)
+    row = lax.rem(me, quarter) // eighth
     loads = [
         pltpu.make_async_copy(s, d, load_sem.at[i])
         for i, (s, d) in enumerate(
             ((ids_hbm, lookups), (grads_hbm, grads), (accum_hbm, accum), (emb_hbm, table))
         )
     ]
+    barrier = pltpu.get_barrier_semaphore()
     for load in loads:
         load.start()
-    barrier = pltpu.get_barrier_semaphore()
     greet_all(barrier, me, n)
 
     loads[0].wait()
@@ -124,7 +138,6 @@
         send_ids[p] = named[p : p + 1, :]
     loads[1].wait()
     fill(sorted_terms, grads[...], width)
-    pl.semaphore_wait(barrier, n - 1)
 
     def rows_of(ref, p):
         return ref.at[pl.ds(pl.multiple_of(p * per_peer, 8), per_peer), :]
@@ -150,15 +163,27 @@
             device_id=(p,), device_id_type=MESH,
         )
 
-    def first_peer(i):
-        cross = 1 - lax.rem(i // 2, 2)
+    def mine(at_inner, at_outer):
+        return inner * at_inner + (1 - inner) * at_outer
+
+    def digit_of(order, i):
+        return lax.rem(lax.shift_right_logical(jnp.int32(order), jnp.int32(3 * i)), 8)
+
+    def first_peer(order, i):
+        piece_at = digit_of(order, i)
+        cross, middle, turn = piece_at // 4, lax.rem(piece_at // 2, 2), lax.rem(piece_at, 2)
         half = cross * (1 - side) + (1 - cross) * side
-        target = quarter_at(half, 1 - i // 4)
-        return target * quarter + lax.rem(lax.rem(me, quarter) // eighth + i, 2) * eighth
-
-    def start_piece(copy, i):
+        return quarter_at(half, middle) * quarter + lax.rem(row + turn, 2) * eighth
+
+    def first_out(i):
+        return first_peer(OUT, i)
+
+    def first_back(i):
+        return first_peer(mine(BACK_INNER, BACK_OUTER), i)
+
+    def start_piece(copy, first, i):
         def start(s, carry):
-            p = first_peer(i) + lax.rem(lax.rem(me, eighth) + s, eighth)
+            p = first(i) + lax.rem(lax.rem(me, eighth) + s, eighth)
 
             @pl.when(p != me)
             def _():
@@ -169,7 +194,7 @@
         lax.fori_loop(0, eighth, start, 0)
 
     def arrange(i):
-        begin = pl.multiple_of(first_peer(i) * per_peer, piece)
+        begin = pl.multiple_of(first_out(i) * per_peer, piece)
         place = begin + lax.broadcasted_iota(jnp.int32, (piece, LANES), 0)
         pick = jnp.concatenate([one_hot_bf16(place == p) for p in pos], axis=1)
         send[pl.ds(begin, piece), :] = joined(dot(pick, sorted_terms[...]), width)
@@ -179,12 +204,15 @@
         return carry
 
     arrange(0)
+    pl.semaphore_wait(barrier, n - 1)
     lax.fori_loop(1, n, start_ids, 0)
-
-    @pl.loop(1, 8)
+    start_piece(grads_copy, first_out, 0)
+    arrange(1)
+
+    @pl.loop(2, 8)
     def _(i):
         arrange(i)
-        start_piece(grads_copy, i - 1)
+        start_piece(grads_copy, first_out, i - 1)
 
     recv_ids[pl.ds(me, 1)] = send_ids[pl.ds(me, 1)]
 
@@ -194,10 +222,11 @@
         return carry
 
     lax.fori_loop(1, n, ids_arrive, 0)
-    start_piece(grads_copy, 7)
+    start_piece(grads_copy, first_out, 7)
     rows_of(recv, me)[...] = rows_of(send, me)[...]
     for b in range(blocks):
-        ids_ref[b : b + 1, :] = sum(recv_ids[b * per_row + k] for k in range(per_row))
+        line = sum(recv_ids[b * per_row + k] for k in range(per_row))
+        ids_ref[b : b + 1, :] = jnp.clip(line, 0, rows_dev - 1)
     to_smem = pltpu.make_async_copy(ids_ref, ids_smem, smem_sem)
     to_smem.start()
 
@@ -209,6 +238,7 @@
     loads[2].wait()
     acc3 = jnp.concatenate(split3(accum[...]), axis=1)
     terms[:, 3 * width : 4 * width] = jnp.ones((tile, width), BF16)
+
     to_smem.wait()
     loads[3].wait()
 
@@ -216,47 +246,74 @@
     def _(b):
         start = pl.multiple_of(b * LANES, LANES)
         for i in range(0, LANES, BATCH):
-            picks = [jnp.clip(ids_smem[b, i + k], 0, rows_dev - 1) for k in range(BATCH)]
-            batch = [table[pl.ds(pick, 1), :] for pick in picks]
+            batch = [table[pl.ds(ids_smem[b, i + k], 1), :] for k in range(BATCH)]
             for k in range(BATCH):
                 old_rows[pl.ds(start + i + k, 1), :] = batch[k]
 
-    acc[...] = jnp.zeros_like(acc)
-
-    @pl.loop(0, 4)
-    def _(i):
-        half = (i // 2) * (1 - side) + (1 - i // 2) * side
-        source = 2 * half + lax.rem(me // quarter + i, 2)
-
-        def arrive(s, carry):
-            p = source * quarter + s
-
-            @pl.when(p != me)
-            def _():
-                grads_copy(p, p).wait_recv()
-
-            return carry
-
-        lax.fori_loop(0, quarter, arrive, 0)
-        fill(terms, recv[pl.ds(pl.multiple_of(source * tile, tile), tile), :], width)
-        lines = tile // LANES
-        rows = [ids_ref[pl.ds(source * lines + k, 1), :] for k in range(lines)]
+    lines = piece // LANES
+    other = 2 * side + 1 - lax.rem(floor, 2)
+    near, far = quarter_at(1 - side, 1), quarter_at(1 - side, 0)
+
+    def receive(pieces):
+        rows = []
+        for k, source in enumerate(pieces):
+
+            def arrive(s, carry, source=source):
+                p = source * eighth + s
+
+                @pl.when(p != me)
+                def _():
+                    grads_copy(p, p).wait_recv()
+
+                return carry
+
+            lax.fori_loop(0, eighth, arrive, 0)
+            begin = pl.multiple_of(source * piece, piece)
+            fill(terms.at[k * piece : (k + 1) * piece, :], recv[pl.ds(begin, piece), :], width)
+            rows += [ids_ref[pl.ds(source * lines + j, 1), :] for j in range(lines)]
+        return rows
+
+    def added(here, rows):
+        col = cols[here, :]
+        same = jnp.concatenate([one_hot_bf16(col == r) for r in rows], axis=1)
+        return dot(same, terms[...])
+
+    def pieces_at(i):
+        group = digit_of(mine(IN_INNER, IN_OUTER), i)
+        cross, odd = group // 2, lax.rem(group, 2)
+        whole = floor * (1 - odd) + other * odd
+        turn = row * (1 - odd) + (1 - row) * odd
+        return [
+            (1 - cross) * 2 * whole + cross * (2 * near + turn),
+            (1 - cross) * (2 * whole + 1) + cross * (2 * far + turn),
+        ]
+
+    def add_source(i):
+        rows = receive(pieces_at(i))
 
         @pl.loop(0, 4)
         def _(t):
             here = pl.ds(pl.multiple_of(t * tile, tile), tile)
-            col = cols[here, :]
-            same = jnp.concatenate([one_hot_bf16(col == r) for r in rows], axis=1)
-            acc[here, :] += dot(same, terms[...])
-
+            if isinstance(i, int):
+                acc[here, :] = added(here, rows)
+            else:
+                acc[here, :] += added(here, rows)
+
+    add_source(0)
+
+    @pl.loop(1, 3)
+    def _(i):
+        add_source(i)
+
+    last = receive(pieces_at(3))
     lane = lax.broadcasted_iota(jnp.int32, (piece, LANES), 1)
     group_iota = lax.broadcasted_iota(jnp.int32, (piece, groups), 1)
 
     @pl.loop(0, 8)
     def _(i):
-        here = pl.ds(pl.multiple_of(first_peer(i) * per_peer, piece), piece)
+        here = pl.ds(pl.multiple_of(first_back(i) * per_peer, piece), piece)
         col = cols[here, :]
-        out = acc[here, :]
+        out = acc[here, :] + added(here, last)
         summed = joined(out, width)
         times = out[:, 3 * width : 3 * width + 1]
         mean = jnp.sum(summed * summed, axis=1, keepdims=True) * (1.0 / width)
@@ -273,13 +330,13 @@
 
         @pl.when(i > 0)
         def _():
-            start_piece(back_copy, i - 1)
-
-    added = lax.dot_general(
+            start_piece(back_copy, first_back, i - 1)
+
+    means = lax.dot_general(
         hi_hot[...], weights[...], (((0,), (0,)), ((), ())), preferred_element_type=F32
     )
-    new_accum_ref[...] = accum[...] + joined(added, LANES)
-    start_piece(back_copy, 7)
+    new_accum_ref[...] = accum[...] + joined(means, LANES)
+    start_piece(back_copy, first_back, 7)
     rows_of(back, me)[...] = rows_of(fresh, me)[...]
 
     def back_arrive(step, carry):

time: 68.2 us -> 62.1 us (0.911); the launches traced: 68 us -> 60.9 us
  Pallas kernels: 67.4 us -> 60.3 us
    pallas_call x1, Pallas kernels: 61.1 us -> 54 us  [on_device(): pl.pallas_call(functools.partial(step_kernel, n), out_shape=[pltpu.VMEM((...]
where the time goes in v2:
time: 62.1 us; the launch traced here: 60.9 us
  Pallas kernels  60.3 us (97%)
  between operations  0.64 us (1%)
    pallas_call x1, Pallas kernels, on_device(): pl.pallas_call(functools.partial(step_kernel, n), out_shape=[pltpu.VMEM((...  54 us
    pallas_call x1, Pallas kernels, on_device(): pl.pallas_call(finish_kernel, out_shape=[jax.ShapeDtypeStruct((rows_dev,...  6.24 us

profile of v2, /device:TPU:0, one launch (start us, length us, event | category | flops | bytes accessed | tf_op | source)
XLA Modules:
  0.0 60.9 jit_solution(3647447223447969515)
XLA Ops:
  0.6 54.0 %shard_map.67 = (s32[16,128]{1,0:T(8,128)S(1)}, s32[16,128]{1,0:T(8,128)S(1)}, f32[2048,128]{1,0:T(8,128)S(1)}, f32[128,128]{1,0:T(8,128)S(1)}, f32[16384,128]{1,0:T(8,128)S(1)}, /*index=5*/f32[2048,128]{1,0:T(8,128)S(1)}) custom-call(s32[16,128]{1,0:T(8,128)} %bitcast.4, f32[2048,128]{1,0:T(8,128)} %grads_hbm.1, f32[128,128]{1,0:T(8,128)} %bitcast.3, ...), custom_call_target="tpu_custom_call" | custom-call | tf_op jit(solution)/shard_map/pallas_call | solution.py:424
  54.7 6.2 %shard_map.68 = (f32[16384,128]{1,0:T(8,128)}, f32[128,128]{1,0:T(8,128)}, f32[2048,128]{1,0:T(8,128)}, f32[16384,128]{1,0:T(8,128)S(1)}) custom-call(s32[16,128]{1,0:T(8,128)S(1)} %get-tuple-element.12.pos_smem, s32[16,128]{1,0:T(8,128)S(1)} %get-tuple-element.13.ids_smem, ...), custom_call_target="tpu_custom_call", output_to_operand_aliasing={{3}: (5, {})} | custom-call | tf_op jit(solution)/shard_map/pallas_call | solution.py:471

commit v3 on v2

--- a/solution.py
+++ b/solution.py
@@ -145,23 +145,27 @@
     def ids_copy(p, source):
         return pltpu.make_async_remote_copy(
             src_ref=send_ids.at[p], dst_ref=recv_ids.at[source],
-            send_sem=ids_out.at[p], recv_sem=ids_in.at[source],
+            send_sem=ids_out, recv_sem=ids_in,
             device_id=(p,), device_id_type=MESH,
         )
 
     def grads_copy(p, source):
         return pltpu.make_async_remote_copy(
             src_ref=rows_of(send, p), dst_ref=rows_of(recv, source),
-            send_sem=grads_out.at[p], recv_sem=grads_in.at[source],
+            send_sem=grads_out, recv_sem=grads_in.at[source // eighth],
             device_id=(p,), device_id_type=MESH,
         )
 
     def back_copy(p, source):
         return pltpu.make_async_remote_copy(
             src_ref=rows_of(fresh, p), dst_ref=rows_of(back, source),
-            send_sem=back_out.at[p], recv_sem=back_in.at[source],
+            send_sem=back_out, recv_sem=back_in,
             device_id=(p,), device_id_type=MESH,
         )
+
+    def wait_rows(ref, begin, rows, sem):
+        here = ref.at[pl.ds(begin, rows), :]
+        pltpu.make_async_copy(here, here, sem).wait()
 
     def mine(at_inner, at_outer):
         return inner * at_inner + (1 - inner) * at_outer
@@ -216,12 +220,8 @@
 
     recv_ids[pl.ds(me, 1)] = send_ids[pl.ds(me, 1)]
 
-    def ids_arrive(step, carry):
-        p = lax.rem(me + step, n)
-        ids_copy(p, p).wait_recv()
-        return carry
-
-    lax.fori_loop(1, n, ids_arrive, 0)
+    others = recv_ids.at[pl.ds(0, n - 1)]
+    pltpu.make_async_copy(others, others, ids_in).wait()
     start_piece(grads_copy, first_out, 7)
     rows_of(recv, me)[...] = rows_of(send, me)[...]
     for b in range(blocks):
@@ -258,17 +258,16 @@
         rows = []
         for k, source in enumerate(pieces):
 
-            def arrive(s, carry, source=source):
-                p = source * eighth + s
-
-                @pl.when(p != me)
-                def _():
-                    grads_copy(p, p).wait_recv()
-
-                return carry
-
-            lax.fori_loop(0, eighth, arrive, 0)
             begin = pl.multiple_of(source * piece, piece)
+
+            @pl.when(source == me // eighth)
+            def _(begin=begin, source=source):
+                wait_rows(recv, begin, piece - per_peer, grads_in.at[source])
+
+            @pl.when(source != me // eighth)
+            def _(begin=begin, source=source):
+                wait_rows(recv, begin, piece, grads_in.at[source])
+
             fill(terms.at[k * piece : (k + 1) * piece, :], recv[pl.ds(begin, piece), :], width)
             rows += [ids_ref[pl.ds(source * lines + j, 1), :] for j in range(lines)]
         return rows
@@ -339,21 +338,10 @@
     start_piece(back_copy, first_back, 7)
     rows_of(back, me)[...] = rows_of(fresh, me)[...]
 
-    def back_arrive(step, carry):
-        p = lax.rem(me + step, n)
-        back_copy(p, p).wait_recv()
-        return carry
-
-    lax.fori_loop(1, n, back_arrive, 0)
-
-    def drain(step, carry):
-        p = lax.rem(me + step, n)
-        ids_copy(p, me).wait_send()
-        grads_copy(p, me).wait_send()
-        back_copy(p, me).wait_send()
-        return carry
-
-    lax.fori_loop(1, n, drain, 0)
+    wait_rows(back, 0, look - per_peer, back_in)
+    pltpu.make_async_copy(others, others, ids_out).wait()
+    wait_rows(send, 0, look - per_peer, grads_out)
+    wait_rows(fresh, 0, look - per_peer, back_out)
 
 
 def finish_kernel(
@@ -451,12 +439,12 @@
             pltpu.SMEM((blocks, LANES), jnp.int32),
             dma((4,)),
             dma(()),
-            dma((n,)),
-            dma((n,)),
-            dma((n,)),
-            dma((n,)),
-            dma((n,)),
-            dma((n,)),
+            dma(()),
+            dma(()),
+            dma(()),
+            dma((8,)),
+            dma(()),
+            dma(()),
         ],
         compiler_params=pltpu.CompilerParams(
             collective_id=1, has_side_effects=True, vmem_limit_bytes=44 * MIB

time: 62.1 us -> 60.1 us (0.968)
  Pallas kernels: 60.3 us -> 58.3 us
    pallas_call x1, Pallas kernels: 54 us -> 52.1 us  [on_device(): pl.pallas_call(functools.partial(step_kernel, n), out_shape=[pltpu.VMEM((...]
where the time goes in v3:
time: 60.1 us; the launch traced here: 59 us
  Pallas kernels  58.3 us (97%)
  between operations  0.64 us (1%)
    pallas_call x1, Pallas kernels, on_device(): pl.pallas_call(functools.partial(step_kernel, n), out_shape=[pltpu.VMEM((...  52.1 us
    pallas_call x1, Pallas kernels, on_device(): pl.pallas_call(finish_kernel, out_shape=[jax.ShapeDtypeStruct((rows_dev,...  6.24 us

profile of v3, /device:TPU:0, one launch (start us, length us, event | category | flops | bytes accessed | tf_op | source)
XLA Modules:
  0.0 59.0 jit_solution(9096471840499441887)
XLA Ops:
  0.6 52.1 %shard_map.67 = (s32[16,128]{1,0:T(8,128)S(1)}, s32[16,128]{1,0:T(8,128)S(1)}, f32[2048,128]{1,0:T(8,128)S(1)}, f32[128,128]{1,0:T(8,128)S(1)}, f32[16384,128]{1,0:T(8,128)S(1)}, /*index=5*/f32[2048,128]{1,0:T(8,128)S(1)}) custom-call(s32[16,128]{1,0:T(8,128)} %bitcast.4, f32[2048,128]{1,0:T(8,128)} %grads_hbm.1, f32[128,128]{1,0:T(8,128)} %bitcast.3, ...), custom_call_target="tpu_custom_call" | custom-call | tf_op jit(solution)/shard_map/pallas_call | solution.py:412
  52.7 6.2 %shard_map.68 = (f32[16384,128]{1,0:T(8,128)}, f32[128,128]{1,0:T(8,128)}, f32[2048,128]{1,0:T(8,128)}, f32[16384,128]{1,0:T(8,128)S(1)}) custom-call(s32[16,128]{1,0:T(8,128)S(1)} %get-tuple-element.12.pos_smem, s32[16,128]{1,0:T(8,128)S(1)} %get-tuple-element.13.ids_smem, ...), custom_call_target="tpu_custom_call", output_to_operand_aliasing={{3}: (5, {})} | custom-call | tf_op jit(solution)/shard_map/pallas_call | solution.py:459

commit v4 on v3

--- a/solution.py
+++ b/solution.py
@@ -12,6 +12,7 @@
 LANES = 128
 MIB = 1024 * 1024
 BATCH = 16
+SEGMENTS = 8
 MESH = pl.DeviceIdType.MESH
 
 
@@ -73,9 +74,9 @@
 
 def step_kernel(
     n, ids_hbm, grads_hbm, accum_hbm, emb_hbm,
-    pos_ref, ids_ref, fresh, new_accum_ref, table, back,
-    lookups, grads, accum, send_ids, send, recv_ids, recv, sorted_terms, terms, acc, cols, old_rows,
-    weights, hi_hot, ids_smem,
+    plan, fresh, new_accum_ref, table, back,
+    ids_ref, lookups, grads, accum, send_ids, send, recv_ids, recv, sorted_terms, terms, acc, cols, old_rows,
+    weights, hi_hot, prior, ids_smem,
     load_sem, smem_sem, ids_out, ids_in, grads_out, grads_in, back_out, back_in,
 ):
     blocks = lookups.shape[0]
@@ -87,6 +88,7 @@
     per_row = LANES // per_peer
     quarter = n // 4
     eighth = n // 8
+    low_rows = rows_dev // SEGMENTS
     piece = look // 8
     tile = look // 4
     me = lax.axis_index("shard")
@@ -101,9 +103,11 @@
         )
     ]
     barrier = pltpu.get_barrier_semaphore()
-    for load in loads:
+    for load in loads[:2]:
         load.start()
     greet_all(barrier, me, n)
+    for load in loads[2:]:
+        load.start()
 
     loads[0].wait()
     peer_iota = lax.broadcasted_iota(jnp.int32, (n, LANES), 0)
@@ -121,7 +125,7 @@
         rank = jnp.sum(hot * rank, axis=0, keepdims=True).astype(jnp.int32)
         peer = jnp.sum(jnp.where(mine, peer_iota, 0), axis=0, keepdims=True)
         pos.append(peer * per_peer + rank)
-        pos_ref[b : b + 1, :] = pos[b]
+        plan[b : b + 1, :] = pos[b]
         base = base + jnp.sum(hot, axis=1, keepdims=True)
         offset = ids - peer * rows_dev
         digits = [offset & 255, (offset >> 8) & 255, offset >> 16]
@@ -250,6 +254,19 @@
             for k in range(BATCH):
                 old_rows[pl.ds(start + i + k, 1), :] = batch[k]
 
+    lane = lax.broadcasted_iota(jnp.int32, (piece, LANES), 1)
+    group_iota = lax.broadcasted_iota(jnp.int32, (piece, groups), 1)
+
+    @pl.loop(0, 8)
+    def _(i):
+        here = pl.ds(pl.multiple_of(i * piece, piece), piece)
+        col = cols[here, :]
+        at_lane = (col & (LANES - 1)) == lane
+        at_group = one_hot_bf16((col >> 7)[:, 0:1] == group_iota)
+        hi_hot[here, :] = at_group
+        found = joined(dot(at_group, acc3), LANES)
+        prior[here, :] = jnp.sum(jnp.where(at_lane, found, 0.0), axis=1, keepdims=True)
+
     lines = piece // LANES
     other = 2 * side + 1 - lax.rem(floor, 2)
     near, far = quarter_at(1 - side, 1), quarter_at(1 - side, 0)
@@ -305,38 +322,83 @@
         add_source(i)
 
     last = receive(pieces_at(3))
-    lane = lax.broadcasted_iota(jnp.int32, (piece, LANES), 1)
-    group_iota = lax.broadcasted_iota(jnp.int32, (piece, groups), 1)
-
     @pl.loop(0, 8)
     def _(i):
         here = pl.ds(pl.multiple_of(first_back(i) * per_peer, piece), piece)
-        col = cols[here, :]
         out = acc[here, :] + added(here, last)
+        acc[here, :] = out
         summed = joined(out, width)
-        times = out[:, 3 * width : 3 * width + 1]
         mean = jnp.sum(summed * summed, axis=1, keepdims=True) * (1.0 / width)
-        at_lane = (col & (LANES - 1)) == lane
-        at_group = one_hot_bf16((col >> 7)[:, 0:1] == group_iota)
-        found = joined(dot(at_group, acc3), LANES)
-        new_acc = jnp.sum(jnp.where(at_lane, found, 0.0), axis=1, keepdims=True) + mean
-        rate = LEARNING_RATE / (jnp.sqrt(new_acc) + EPSILON)
-        fresh[here, :] = old_rows[here, :] - summed * rate
-        share = jnp.where(at_lane, jnp.broadcast_to(mean / times, (piece, LANES)), 0.0)
-        for k, term in enumerate(split3(share)):
-            weights[here, k * LANES : (k + 1) * LANES] = term
-        hi_hot[here, :] = at_group
+        rate = LEARNING_RATE / (jnp.sqrt(prior[here, :] + mean) + EPSILON)
+        step = summed * rate
+        fresh[here, :] = old_rows[here, :] - step
+        old_rows[here, :] = step
 
         @pl.when(i > 0)
         def _():
             start_piece(back_copy, first_back, i - 1)
+
+    rows_of(back, me)[...] = rows_of(fresh, me)[...]
+
+    @pl.loop(0, 8)
+    def _(i):
+        here = pl.ds(pl.multiple_of(i * piece, piece), piece)
+
+        @pl.when(i == 1)
+        def _():
+            start_piece(back_copy, first_back, 7)
+
+        out = acc[here, :]
+        summed = joined(out, width)
+        mean = jnp.sum(summed * summed, axis=1, keepdims=True) * (1.0 / width)
+        part = 1.0 / out[:, 3 * width : 3 * width + 1]
+        fill(sorted_terms.at[here, :], old_rows[here, :] * part, width)
+        at_lane = (cols[here, :] & (LANES - 1)) == lane
+        share = jnp.where(at_lane, jnp.broadcast_to(mean * part, (piece, LANES)), 0.0)
+        for k, term in enumerate(split3(share)):
+            weights[here, k * LANES : (k + 1) * LANES] = term
 
     means = lax.dot_general(
         hi_hot[...], weights[...], (((0,), (0,)), ((), ())), preferred_element_type=F32
     )
     new_accum_ref[...] = accum[...] + joined(means, LANES)
-    start_piece(back_copy, first_back, 7)
-    rows_of(back, me)[...] = rows_of(fresh, me)[...]
+
+    base = jnp.zeros((1, 1), F32)
+    line_iota = lax.broadcasted_iota(jnp.int32, (blocks, LANES), 0)
+    lane_row = lax.broadcasted_iota(jnp.int32, (1, LANES), 1)
+    owned, ranked = [], []
+    for b in range(blocks):
+        line = ids_ref[b : b + 1, :]
+        high = jnp.where(line >= low_rows, 1.0, 0.0)
+        place = jnp.where(line >= low_rows, dot(high.astype(BF16), before) + base, -1.0)
+        place = place.astype(jnp.int32)
+        base = base + jnp.sum(high, axis=1, keepdims=True)
+        hot = jnp.where(line_iota == place >> 7, 1.0, 0.0)
+        digits = [line & 255, (line >> 8) & 255, line >> 16, lane_row, jnp.full_like(line, b)]
+        digits.append(jnp.ones_like(line))
+        owned.append(jnp.concatenate([hot * d.astype(F32) for d in digits], axis=0).astype(BF16))
+        ranked.append(one_hot_bf16((slot_iota == place & (LANES - 1)) & (place >= 0)))
+    listed = lax.dot_general(
+        jnp.concatenate(owned, axis=1),
+        jnp.concatenate(ranked, axis=1),
+        (((1,), (1,)), ((), ())),
+        preferred_element_type=F32,
+    ).astype(jnp.int32)
+    named = [listed[i * blocks : (i + 1) * blocks] for i in range(6)]
+    high_rows = named[0] + named[1] * 256 + named[2] * 65536
+    both = high_rows * look + named[3] + named[4] * LANES
+    both = jnp.where(named[5] > 0, both, jnp.broadcast_to(both[0:1, 0:1], (blocks, LANES)))
+    total = jnp.broadcast_to(base.astype(jnp.int32), (8, LANES))
+    plan[blocks :, :] = jnp.concatenate([total[0:1], both, total[1:]], axis=0)
+    rows = [ids_ref[b : b + 1, :] for b in range(blocks)]
+
+    @pl.loop(0, low_rows // piece)
+    def _(i):
+        begin = pl.multiple_of(i * piece, piece)
+        here = pl.ds(begin, piece)
+        place = begin + lax.broadcasted_iota(jnp.int32, (piece, LANES), 0)
+        pick = jnp.concatenate([one_hot_bf16(place == r) for r in rows], axis=1)
+        table[here, :] -= joined(dot(pick, sorted_terms[...]), width)
 
     wait_rows(back, 0, look - per_peer, back_in)
     pltpu.make_async_copy(others, others, ids_out).wait()
@@ -345,27 +407,55 @@
 
 
 def finish_kernel(
-    pos_smem, ids_smem, fresh, back, accum, table_in,
+    plan_ref, fresh, back, accum, table_in,
     new_table, new_accum, looked_up, table,
-    rows, table_sem, accum_sem, rows_sem,
+    rows, plan, plan_sem, table_sem, accum_sem, rows_sem,
 ):
     del table_in
     look = fresh.shape[0]
     blocks = look // LANES
     tile = look // 4
+    segment = table.shape[0] // SEGMENTS
+    def read(part, begin, count):
+        here = pl.ds(begin, count)
+        return pltpu.make_async_copy(plan_ref.at[here, :], plan.at[here, :], plan_sem.at[part])
+
+    head, tail, order = read(0, blocks, 8), read(1, blocks + 8, blocks), read(2, 0, blocks)
+    head.start()
     keep = pltpu.make_async_copy(accum, new_accum, accum_sem)
     keep.start()
 
-    @pl.loop(0, blocks)
-    def _(b):
-        start = pl.multiple_of(b * LANES, LANES)
-        for i in range(0, LANES, BATCH):
-            batch = [fresh[pl.ds(start + i + k, 1), :] for k in range(BATCH)]
-            for k in range(BATCH):
-                table[pl.ds(ids_smem[b, i + k], 1), :] = batch[k]
-
-    store = pltpu.make_async_copy(table, new_table, table_sem)
-    store.start()
+    def store(i):
+        here = pl.ds(pl.multiple_of(i * segment, segment), segment)
+        return pltpu.make_async_copy(table.at[here, :], new_table.at[here, :], table_sem.at[i])
+
+    store(0).start()
+    head.wait()
+    order.start()
+    lines = (plan[blocks, 0] + LANES - 1) // LANES
+
+    shift = look.bit_length() - 1
+
+    def scatter(begin, end):
+        @pl.loop(begin, end)
+        def _(b):
+            for i in range(0, LANES, BATCH):
+                both = [plan[blocks + 1 + b, i + k] for k in range(BATCH)]
+                batch = [fresh[pl.ds(v & (look - 1), 1), :] for v in both]
+                for v, values in zip(both, batch):
+                    table[pl.ds(v >> shift, 1), :] = values
+
+    scatter(0, jnp.minimum(lines, 7))
+
+    @pl.when(lines > 7)
+    def _():
+        tail.start()
+        tail.wait()
+        scatter(7, lines)
+
+    for i in range(1, SEGMENTS):
+        store(i).start()
+    order.wait()
 
     def out_copy(t):
         here = pl.ds(pl.multiple_of(t * tile, tile), tile)
@@ -378,7 +468,7 @@
             b = t * (tile // LANES) + j
             start = pl.multiple_of(b * LANES, LANES)
             for i in range(0, LANES, BATCH):
-                batch = [back[pl.ds(pos_smem[b, i + k], 1), :] for k in range(BATCH)]
+                batch = [back[pl.ds(plan[b, i + k], 1), :] for k in range(BATCH)]
                 for k in range(BATCH):
                     rows[pl.ds(start + i + k, 1), :] = batch[k]
 
@@ -390,7 +480,8 @@
     out_copy(3).start()
     for t in range(4):
         out_copy(t).wait()
-    store.wait()
+    for i in range(SEGMENTS):
+        store(i).wait()
 
 
 def in_hbm(x):
@@ -404,24 +495,23 @@
     blocks = look // LANES
     groups = rows_dev // LANES
     vmem = pl.BlockSpec(memory_space=pltpu.VMEM)
-    smem = pl.BlockSpec(memory_space=pltpu.SMEM)
     hbm = pl.BlockSpec(memory_space=pltpu.HBM)
     tile = look // 4
     dma = pltpu.SemaphoreType.DMA
 
-    pos, local_ids, fresh, accum, table, back = pl.pallas_call(
+    plan, fresh, accum, table, back = pl.pallas_call(
         functools.partial(step_kernel, n),
         out_shape=[
-            pltpu.VMEM((blocks, LANES), jnp.int32),
-            pltpu.VMEM((blocks, LANES), jnp.int32),
+            pltpu.VMEM((2 * blocks + 8, LANES), jnp.int32),
             pltpu.VMEM((look, width), F32),
             pltpu.VMEM((groups, LANES), F32),
             pltpu.VMEM((rows_dev, width), F32),
             pltpu.VMEM((look, width), F32),
         ],
         in_specs=[hbm] * 4,
-        out_specs=[vmem] * 6,
+        out_specs=[vmem] * 5,
         scratch_shapes=[
+            pltpu.VMEM((blocks, LANES), jnp.int32),
             pltpu.VMEM((blocks, LANES), jnp.int32),
             pltpu.VMEM((look, width), F32),
             pltpu.VMEM((groups, LANES), F32),
@@ -436,6 +526,7 @@
             pltpu.VMEM((look, width), F32),
             pltpu.VMEM((look, 3 * LANES), BF16),
             pltpu.VMEM((look, groups), BF16),
+            pltpu.VMEM((look, 1), F32),
             pltpu.SMEM((blocks, LANES), jnp.int32),
             dma((4,)),
             dma(()),
@@ -464,12 +555,19 @@
             jax.ShapeDtypeStruct((look, width), F32),
             pltpu.VMEM((rows_dev, width), F32),
         ],
-        in_specs=[smem, smem, vmem, vmem, vmem, vmem],
+        in_specs=[vmem] * 5,
         out_specs=[hbm, hbm, hbm, vmem],
-        input_output_aliases={5: 3},
-        scratch_shapes=[pltpu.VMEM((look, width), F32), dma(()), dma(()), dma((4,))],
+        input_output_aliases={4: 3},
+        scratch_shapes=[
+            pltpu.VMEM((look, width), F32),
+            pltpu.SMEM((2 * blocks + 8, LANES), jnp.int32),
+            dma((3,)),
+            dma((SEGMENTS,)),
+            dma(()),
+            dma((4,)),
+        ],
         compiler_params=pltpu.CompilerParams(vmem_limit_bytes=24 * MIB),
-    )(pos, local_ids, fresh, back, accum, table)
+    )(plan, fresh, back, accum, table)
     return (new_table, new_accum.reshape(rows_dev), looked_up)
 
 

time: 60.1 us -> 58.2 us (0.968)
  Pallas kernels: 58.3 us -> 56.7 us
    pallas_call x1, Pallas kernels: 6.24 us -> 4.86 us  [on_device(): pl.pallas_call(finish_kernel, out_shape=[jax.ShapeDtypeStruct((rows_dev,...]
where the time goes in v4:
time: 58.2 us; the launch traced here: 57.3 us
  Pallas kernels  56.7 us (97%)
  between operations  0.64 us (1%)
    pallas_call x1, Pallas kernels, on_device(): pl.pallas_call(functools.partial(step_kernel, n), out_shape=[pltpu.VMEM((...  51.8 us
    pallas_call x1, Pallas kernels, on_device(): pl.pallas_call(finish_kernel, out_shape=[jax.ShapeDtypeStruct((rows_dev,...  4.86 us

profile of v4, /device:TPU:0, one launch (start us, length us, event | category | flops | bytes accessed | tf_op | source)
XLA Modules:
  0.0 57.3 jit_solution(12318378637417772303)
XLA Ops:
  0.6 51.8 %shard_map.67 = (s32[40,128]{1,0:T(8,128)S(1)}, f32[2048,128]{1,0:T(8,128)S(1)}, f32[128,128]{1,0:T(8,128)S(1)}, f32[16384,128]{1,0:T(8,128)S(1)}, f32[2048,128]{1,0:T(8,128)S(1)}) custom-call(s32[16,128]{1,0:T(8,128)} %bitcast.4, f32[2048,128]{1,0:T(8,128)} %grads_hbm.1, f32[128,128]{1,0:T(8,128)} %bitcast.3, f32[16384,128]{1,0:T(8,128)} %emb_hbm.1), custom_call_target="tpu_custom_call" | custom-call | tf_op jit(solution)/shard_map/pallas_call | solution.py:502
  52.4 4.9 %shard_map.68 = (f32[16384,128]{1,0:T(8,128)}, f32[128,128]{1,0:T(8,128)}, f32[2048,128]{1,0:T(8,128)}, f32[16384,128]{1,0:T(8,128)S(1)}) custom-call(s32[40,128]{1,0:T(8,128)S(1)} %get-tuple-element.11.plan_ref, f32[2048,128]{1,0:T(8,128)S(1)} %get-tuple-element.12.fresh, f32[2048,128]{1,0:T(8,128)S(1)} %get-tuple-element.13.back, ...), custom_call_target="tpu_custom_call", output_to_operand_aliasing={{3}: (4, {})} | custom-call | tf_op jit(solution)/shard_map/pallas_call | solution.py:550

commit v5 on v4

--- a/solution.py
+++ b/solution.py
@@ -24,7 +24,7 @@
 IN_INNER = order_of(2, 3, 1, 0)
 IN_OUTER = order_of(0, 1, 2, 3)
 BACK_INNER = order_of(4, 6, 0, 5, 7, 1, 2, 3)
-BACK_OUTER = order_of(2, 3, 4, 6, 5, 7, 0, 1)
+BACK_OUTER = order_of(2, 3, 4, 5, 6, 7, 0, 1)
 F32 = jnp.float32
 BF16 = jnp.bfloat16
 
@@ -88,7 +88,6 @@
     per_row = LANES // per_peer
     quarter = n // 4
     eighth = n // 8
-    low_rows = rows_dev // SEGMENTS
     piece = look // 8
     tile = look // 4
     me = lax.axis_index("shard")
@@ -96,6 +95,7 @@
     floor = me // quarter
     inner = lax.rem(floor + side, 2)
     row = lax.rem(me, quarter) // eighth
+    low_rows = (1 + 2 * inner) * (rows_dev // SEGMENTS)
     loads = [
         pltpu.make_async_copy(s, d, load_sem.at[i])
         for i, (s, d) in enumerate(

time: 58.2 us -> 58 us (level)
  the two profiles are of different devices: /device:TPU:0 before, /device:TPU:9 now
where the time goes in v5:
time: 58 us; the launch traced here: 57.8 us
  Pallas kernels  57.1 us (98%)
  between operations  0.64 us (1%)
    pallas_call x1, Pallas kernels, on_device(): pl.pallas_call(functools.partial(step_kernel, n), out_shape=[pltpu.VMEM((...  52.7 us
    pallas_call x1, Pallas kernels, on_device(): pl.pallas_call(finish_kernel, out_shape=[jax.ShapeDtypeStruct((rows_dev,...  4.45 us

profile of v5, /device:TPU:9, one launch (start us, length us, event | category | flops | bytes accessed | tf_op | source)
XLA Modules:
  0.0 57.8 jit_solution(10491022713963777599)
XLA Ops:
  0.6 52.7 %shard_map.67 = (s32[40,128]{1,0:T(8,128)S(1)}, f32[2048,128]{1,0:T(8,128)S(1)}, f32[128,128]{1,0:T(8,128)S(1)}, f32[16384,128]{1,0:T(8,128)S(1)}, f32[2048,128]{1,0:T(8,128)S(1)}) custom-call(s32[16,128]{1,0:T(8,128)} %bitcast.4, f32[2048,128]{1,0:T(8,128)} %grads_hbm.1, f32[128,128]{1,0:T(8,128)} %bitcast.3, f32[16384,128]{1,0:T(8,128)} %emb_hbm.1), custom_call_target="tpu_custom_call" | custom-call | tf_op jit(solution)/shard_map/pallas_call | solution.py:502
  53.3 4.5 %shard_map.68 = (f32[16384,128]{1,0:T(8,128)}, f32[128,128]{1,0:T(8,128)}, f32[2048,128]{1,0:T(8,128)}, f32[16384,128]{1,0:T(8,128)S(1)}) custom-call(s32[40,128]{1,0:T(8,128)S(1)} %get-tuple-element.11.plan_ref, f32[2048,128]{1,0:T(8,128)S(1)} %get-tuple-element.12.fresh, f32[2048,128]{1,0:T(8,128)S(1)} %get-tuple-element.13.back, ...), custom_call_target="tpu_custom_call", output_to_operand_aliasing={{3}: (4, {})} | custom-call | tf_op jit(solution)/shard_map/pallas_call | solution.py:550
